TPU v7x, 32 devices: a whole 2x2x4 slice. The times are simulated.
32 devices in a mesh: section: 2 (over y), rep: 4 (over z), sub: 4 (over x, core).
Axes of the slice: x: 2, y: 2, z: 4, core: 2. Of those that a mesh axis runs over, the one named last changes fastest.
Arguments:
- token_ids: int32 [8, 512], P(None, ('rep', 'sub')), may hold values from 0 to 255
- target_ids: int32 [8, 512], P(None, ('rep', 'sub')), may hold values from 0 to 255
- embedding: bfloat16 [256, 2048], P(('rep', 'sub')), may hold values from -3 to 3
- section_weight: bfloat16 [2, 2048, 2048], P('section', ('rep', 'sub')), may hold values from -0.125 to 0.125
- section_gain: float32 [2, 2048], P('section'), may hold values from 0.1 to 1.9
- final_gain: float32 [2048], replicated, may hold values from 0.5 to 1.5
Outputs:
- weight_grad: float32 [2, 2048, 2048], P('section', ('rep', 'sub'))
- gain_grad: float32 [2, 2048], P('section')
- embed_grad: float32 [256, 2048], P(('section', 'rep', 'sub'))
- final_grad: float32 [2048], replicated
All inputs are finite; a program needn't handle non-finite values.
Results may differ from a plain program's by a relative error of at most 0.024.
Values may be sent and summed in bfloat16 or wider, within the bound.
A program may use at most 64 MiB of HBM per device.

v0:
```python
import jax
import jax.numpy as jnp
from jax import lax
from jax.sharding import PartitionSpec as P

epsilon = 1e-06
gelu_coef = 0.7978845608028654
cube_coef = 0.044715


def passed_along(value, axis, steps):
    count = lax.axis_size(axis)
    initial, last = (max(0, -steps), min(count, count - steps))
    return lax.ppermute(value, axis, [(source, source + steps) for source in range(initial, last)])


def gelu(pre_act):
    return (
        0.5
        * pre_act
        * (1.0 + jnp.tanh(gelu_coef * (pre_act + cube_coef * pre_act * pre_act * pre_act)))
    )


def gelu_slope(pre_act):
    inside = gelu_coef * (pre_act + cube_coef * pre_act * pre_act * pre_act)
    tangent = jnp.tanh(inside)
    return 0.5 * (1.0 + tangent) + 0.5 * pre_act * (1.0 - tangent * tangent) * gelu_coef * (
        1.0 + 3.0 * cube_coef * pre_act * pre_act
    )


def normalize(residual, gain_row):
    values = residual.astype(jnp.float32)
    scale_inv = lax.rsqrt(jnp.mean(values * values, axis=-1, keepdims=True) + epsilon)
    normed = values * scale_inv
    return (normed, scale_inv, (normed * gain_row).astype(jnp.bfloat16))


def norm_back(grad_norm, normed, scale_inv, gain_row):
    grad_unit = grad_norm * gain_row
    grad_in = scale_inv * (
        grad_unit - normed * jnp.mean(grad_unit * normed, axis=-1, keepdims=True)
    )
    return (grad_in, jnp.sum(grad_norm * normed, axis=0))


def pick_slot(buffer, slot_index):
    return lax.dynamic_index_in_dim(buffer, slot_index, 0, keepdims=False)


def place_slot(buffer, update, slot_index):
    return lax.dynamic_update_index_in_dim(buffer, update, slot_index, 0)


def body(token_ids, target_ids, embedding, section_weight, section_gain, final_gain):
    sections = lax.axis_size("section")
    position = lax.axis_index("section")
    micro_count = token_ids.shape[0]
    row_count = token_ids.shape[1]
    features = embedding.shape[1]
    group_size = lax.axis_size(("rep", "sub"))
    vocab_rows = embedding.shape[0] * group_size
    tick_count = micro_count + sections - 1
    contract_last = (((1,), (1,)), ((), ()))
    contract_first = (((0,), (0,)), ((), ()))
    vocab_table = lax.all_gather(embedding, ("rep", "sub"), axis=0, tiled=True)
    weight = lax.all_gather(section_weight, ("rep", "sub"), axis=1, tiled=True)[0]
    gain_row = section_gain[0]
    is_first = position == 0
    is_last = position == sections - 1
    vocab_iota = jnp.arange(vocab_rows, dtype=jnp.int32)
    onehot_in = (token_ids.reshape(-1)[:, None] == vocab_iota[None, :]).astype(jnp.bfloat16)
    embedded = jnp.dot(onehot_in, vocab_table, preferred_element_type=jnp.float32).astype(
        jnp.bfloat16
    )
    embedded = embedded.reshape(micro_count, row_count, features)
    empty_rows = jnp.zeros((row_count, features), jnp.bfloat16)
    zeros_stash = jnp.zeros((micro_count, row_count, features), jnp.bfloat16)
    zeros_pre = jnp.zeros((micro_count, row_count, features), jnp.float32)

    def forward_tick(carried, tick_index):
        arrived = carried[0]
        buffers = carried[1:]
        offset = tick_index - position
        active = (offset >= 0) & (offset < micro_count)
        slot_index = jnp.clip(offset, 0, micro_count - 1)
        residual = jnp.where(is_first, pick_slot(embedded, slot_index), arrived)

        def forward_compute(kept_activations):
            input_list, rounded_list, preactivation_list, output_list = kept_activations
            normed, scale_inv, rounded = normalize(residual, gain_row)
            pre_act = jnp.dot(rounded, weight, preferred_element_type=jnp.float32)
            returned_value = (residual.astype(jnp.float32) + gelu(pre_act)).astype(jnp.bfloat16)
            kept_activations = (
                place_slot(input_list, residual, slot_index),
                place_slot(rounded_list, rounded, slot_index),
                place_slot(preactivation_list, pre_act, slot_index),
                place_slot(output_list, returned_value, slot_index),
            )
            return (kept_activations, returned_value)

        def forward_bypass(kept_activations):
            return (kept_activations, empty_rows)

        buffers, returned_value = lax.cond(active, forward_compute, forward_bypass, buffers)
        arrived = passed_along(returned_value, "section", 1)
        return ((arrived,) + buffers, None)

    start_state = (empty_rows, zeros_stash, zeros_stash, zeros_pre, zeros_stash)
    final_state, unused_out = lax.scan(
        forward_tick, start_state, jnp.arange(tick_count, dtype=jnp.int32)
    )
    input_list, rounded_list, preactivation_list, output_list = final_state[1:]
    logit_scale = float(features) ** (-0.5)

    def head(finals):
        normed, scale_inv, final_rows = normalize(finals, final_gain)
        logits = (
            lax.dot_general(
                final_rows, vocab_table, contract_last, preferred_element_type=jnp.float32
            )
            * logit_scale
        )
        exp_logit = jnp.exp(logits)
        probability = exp_logit / jnp.sum(exp_logit, axis=-1, keepdims=True)
        onehot_out = (target_ids.reshape(-1)[:, None] == vocab_iota[None, :]).astype(jnp.float32)
        grad_logit = ((probability - onehot_out) * logit_scale).astype(jnp.bfloat16)
        embed_head = lax.dot_general(
            grad_logit, final_rows, contract_first, preferred_element_type=jnp.float32
        )
        grad_final = jnp.dot(grad_logit, vocab_table, preferred_element_type=jnp.float32)
        grad_in, final_part = norm_back(grad_final, normed, scale_inv, final_gain)
        grad_top = grad_in.astype(jnp.bfloat16).reshape(micro_count, row_count, features)
        return (embed_head, grad_top, final_part)

    def no_head(finals):
        return (
            jnp.zeros((vocab_rows, features), jnp.float32),
            zeros_stash,
            jnp.zeros((features,), jnp.float32),
        )

    embed_head, grad_top, final_part = lax.cond(
        is_last, head, no_head, output_list.reshape(-1, features)
    )

    def backward_tick(carried, tick_index):
        arrived = carried[0]
        buffers = carried[1:]
        offset = tick_index - (sections - 1 - position)
        active = (offset >= 0) & (offset < micro_count)
        slot_index = jnp.clip(offset, 0, micro_count - 1)
        grad_out = jnp.where(is_last, pick_slot(grad_top, slot_index), arrived)

        def backward_compute(kept_activations):
            preactivation_gradients, first_row_gradients, gain_accumulated = kept_activations
            grad_float = grad_out.astype(jnp.float32)
            grad_pre = (grad_float * gelu_slope(pick_slot(preactivation_list, slot_index))).astype(
                jnp.bfloat16
            )
            grad_norm = lax.dot_general(
                grad_pre, weight, contract_last, preferred_element_type=jnp.float32
            )
            normed, scale_inv, rounded = normalize(pick_slot(input_list, slot_index), gain_row)
            grad_in, gain_part = norm_back(grad_norm, normed, scale_inv, gain_row)
            sent_output = (grad_float + grad_in).astype(jnp.bfloat16)
            kept_activations = (
                place_slot(preactivation_gradients, grad_pre, slot_index),
                place_slot(first_row_gradients, sent_output, slot_index),
                gain_accumulated + gain_part,
            )
            return (kept_activations, sent_output)

        def backward_bypass(kept_activations):
            return (kept_activations, empty_rows)

        buffers, sent_output = lax.cond(active, backward_compute, backward_bypass, buffers)
        arrived = passed_along(sent_output, "section", -1)
        return ((arrived,) + buffers, None)

    back_state = (empty_rows, zeros_stash, zeros_stash, jnp.zeros((features,), jnp.float32))
    back_final, unused_back = lax.scan(
        backward_tick, back_state, jnp.arange(tick_count, dtype=jnp.int32)
    )
    preactivation_gradients, first_row_gradients, gain_accumulated = back_final[1:]
    pres_flat = preactivation_gradients.reshape(-1, features)
    rounded_flat = rounded_list.reshape(-1, features)
    weight_part = lax.psum_scatter(
        lax.dot_general(
            rounded_flat, pres_flat, contract_first, preferred_element_type=jnp.float32
        ).astype(jnp.bfloat16),
        ("rep", "sub"),
        scatter_dimension=0,
        tiled=True,
    ).astype(jnp.float32)
    gain_total = lax.psum(gain_accumulated, ("rep", "sub"))
    final_total = lax.psum(final_part, ("section", "rep", "sub"))
    embed_in = lax.dot_general(
        onehot_in,
        first_row_gradients.reshape(-1, features),
        contract_first,
        preferred_element_type=jnp.float32,
    )
    contribution = jnp.where(is_first, embed_in, 0.0) + embed_head
    embed_total = lax.psum_scatter(
        contribution, ("section", "rep", "sub"), scatter_dimension=0, tiled=True
    )
    return (weight_part[None], gain_total[None], embed_total, final_total)


def solution(mesh):
    in_specs = (
        P(None, ("rep", "sub")),
        P(None, ("rep", "sub")),
        P(("rep", "sub"), None),
        P("section", ("rep", "sub"), None),
        P("section", None),
        P(),
    )
    out_specs = (
        P("section", ("rep", "sub"), None),
        P("section", None),
        P(("section", "rep", "sub"), None),
        P(),
    )
    return jax.shard_map(body, mesh=mesh, in_specs=in_specs, out_specs=out_specs, check_vma=False)
```

profile of v0, /device:TPU:8, one launch (start us, length us, event | category | flops | bytes accessed | tf_op | source)
XLA Modules:
  0.0 676.6 jit_solution(16691863753000079209)
XLA Ops:
  9.5 38.7 %all-gather.3.cloned.1.call-done = bf16[256,2048]{1,0:T(8,128)(2,1)} async-done(((bf16[16,2048]{1,0:T(8,128)(2,1)}), bf16[256,2048]{1,0:T(8,128)(2,1)}) %all-gather.3.cloned.1.call-update) | async-done | bytes 1048592 | tf_op jit(solution)/shard_map/all_gather | solution.py:67
  48.2 2.7 convolution_convert_fusion
  50.8 73.6 %all-gather.5.cloned.1.call-done = bf16[1,2048,2048]{2,1,0:T(8,128)(2,1)} async-done(((bf16[1,128,2048]{2,1,0:T(8,128)(2,1)}), bf16[1,2048,2048]{2,1,0:T(8,128)(2,1)}) %all-gather.5.cloned.1.call-update) | async-done | bytes 8388624 | tf_op jit(solution)/shard_map/all_gather | solution.py:68
  127.3 136.4 %while.36 = (s32[]{:T(128)}, bf16[32,2048]{1,0:T(8,128)(2,1)S(1)}, bf16[8,32,2048]{2,1,0:T(8,128)(2,1)S(1)}, bf16[8,32,2048]{2,1,0:T(8,128)(2,1)}, f32[8,32,2048...) while((s32[]{:T(128)}, bf16[32,2048]{1,0:T(8,128)(2,1)S(1)}, ...), condition=%wide.region_4.5_spmd, body=%wide.region_0.4_spmd.sunk | while | flops 269877280 | bytes 10897188 | solution.py:111
  128.5 7.4 %conditional.6 = (bf16[8,32,2048]{2,1,0:T(8,128)(2,1)S(1)}, bf16[8,32,2048]{2,1,0:T(8,128)(2,1)}, f32[8,32,2048]{2,1,0:T(8,128)}, bf16[8,32,2048]{2,1,0:T(8,128)(2,1)S(1)}, bf16[32,2048]{1,0:T(8,128)(2,1)S(1)}) conditional(s32[]{:T(128)} %convert_element_type.149, (bf16[8,32,2048]{2,1,0:T(8,128)(2,1)S(1)}, bf16[8,32,2048]{2,1,0:T(8,128)(2,1)}, ...), branch_computations={%region_1.1_spmd, %region_2.3_spmd} | conditional | flops 269877280 | bytes 10372557 | solution.py:106
  129.6 5.6 bitcast_dynamic-update-slice_fusion.1
  137.2 3.4 collective-permute-done
  141.7 7.4 %conditional.6 = (bf16[8,32,2048]{2,1,0:T(8,128)(2,1)S(1)}, bf16[8,32,2048]{2,1,0:T(8,128)(2,1)}, f32[8,32,2048]{2,1,0:T(8,128)}, bf16[8,32,2048]{2,1,0:T(8,128)(2,1)S(1)}, bf16[32,2048]{1,0:T(8,128)(2,1)S(1)}) conditional(s32[]{:T(128)} %convert_element_type.149, (bf16[8,32,2048]{2,1,0:T(8,128)(2,1)S(1)}, bf16[8,32,2048]{2,1,0:T(8,128)(2,1)}, ...), branch_computations={%region_1.1_spmd, %region_2.3_spmd} | conditional | flops 269877280 | bytes 10372557 | solution.py:106
  142.8 5.6 bitcast_dynamic-update-slice_fusion.1
  149.1 4.4 collective-permute-start
  153.5 2.6 collective-permute-done
  157.2 7.4 %conditional.6 = (bf16[8,32,2048]{2,1,0:T(8,128)(2,1)S(1)}, bf16[8,32,2048]{2,1,0:T(8,128)(2,1)}, f32[8,32,2048]{2,1,0:T(8,128)}, bf16[8,32,2048]{2,1,0:T(8,128)(2,1)S(1)}, bf16[32,2048]{1,0:T(8,128)(2,1)S(1)}) conditional(s32[]{:T(128)} %convert_element_type.149, (bf16[8,32,2048]{2,1,0:T(8,128)(2,1)S(1)}, bf16[8,32,2048]{2,1,0:T(8,128)(2,1)}, ...), branch_computations={%region_1.1_spmd, %region_2.3_spmd} | conditional | flops 269877280 | bytes 10372557 | solution.py:106
  158.3 5.6 bitcast_dynamic-update-slice_fusion.1
  164.6 4.4 collective-permute-start
  172.6 7.4 %conditional.6 = (bf16[8,32,2048]{2,1,0:T(8,128)(2,1)S(1)}, bf16[8,32,2048]{2,1,0:T(8,128)(2,1)}, f32[8,32,2048]{2,1,0:T(8,128)}, bf16[8,32,2048]{2,1,0:T(8,128)(2,1)S(1)}, bf16[32,2048]{1,0:T(8,128)(2,1)S(1)}) conditional(s32[]{:T(128)} %convert_element_type.149, (bf16[8,32,2048]{2,1,0:T(8,128)(2,1)S(1)}, bf16[8,32,2048]{2,1,0:T(8,128)(2,1)}, ...), branch_computations={%region_1.1_spmd, %region_2.3_spmd} | conditional | flops 269877280 | bytes 10372557 | solution.py:106
  173.7 5.6 bitcast_dynamic-update-slice_fusion.1
  180.0 4.4 collective-permute-start
  184.4 2.5 collective-permute-done
  188.0 7.4 %conditional.6 = (bf16[8,32,2048]{2,1,0:T(8,128)(2,1)S(1)}, bf16[8,32,2048]{2,1,0:T(8,128)(2,1)}, f32[8,32,2048]{2,1,0:T(8,128)}, bf16[8,32,2048]{2,1,0:T(8,128)(2,1)S(1)}, bf16[32,2048]{1,0:T(8,128)(2,1)S(1)}) conditional(s32[]{:T(128)} %convert_element_type.149, (bf16[8,32,2048]{2,1,0:T(8,128)(2,1)S(1)}, bf16[8,32,2048]{2,1,0:T(8,128)(2,1)}, ...), branch_computations={%region_1.1_spmd, %region_2.3_spmd} | conditional | flops 269877280 | bytes 10372557 | solution.py:106
  189.1 5.6 bitcast_dynamic-update-slice_fusion.1
  195.4 4.3 collective-permute-start
  199.7 2.5 collective-permute-done
  203.3 7.4 %conditional.6 = (bf16[8,32,2048]{2,1,0:T(8,128)(2,1)S(1)}, bf16[8,32,2048]{2,1,0:T(8,128)(2,1)}, f32[8,32,2048]{2,1,0:T(8,128)}, bf16[8,32,2048]{2,1,0:T(8,128)(2,1)S(1)}, bf16[32,2048]{1,0:T(8,128)(2,1)S(1)}) conditional(s32[]{:T(128)} %convert_element_type.149, (bf16[8,32,2048]{2,1,0:T(8,128)(2,1)S(1)}, bf16[8,32,2048]{2,1,0:T(8,128)(2,1)}, ...), branch_computations={%region_1.1_spmd, %region_2.3_spmd} | conditional | flops 269877280 | bytes 10372557 | solution.py:106
  204.4 5.6 bitcast_dynamic-update-slice_fusion.1
  210.7 4.3 collective-permute-start
  215.1 2.5 collective-permute-done
  218.7 7.4 %conditional.6 = (bf16[8,32,2048]{2,1,0:T(8,128)(2,1)S(1)}, bf16[8,32,2048]{2,1,0:T(8,128)(2,1)}, f32[8,32,2048]{2,1,0:T(8,128)}, bf16[8,32,2048]{2,1,0:T(8,128)(2,1)S(1)}, bf16[32,2048]{1,0:T(8,128)(2,1)S(1)}) conditional(s32[]{:T(128)} %convert_element_type.149, (bf16[8,32,2048]{2,1,0:T(8,128)(2,1)S(1)}, bf16[8,32,2048]{2,1,0:T(8,128)(2,1)}, ...), branch_computations={%region_1.1_spmd, %region_2.3_spmd} | conditional | flops 269877280 | bytes 10372557 | solution.py:106
  219.8 5.6 bitcast_dynamic-update-slice_fusion.1
  226.1 4.4 collective-permute-start
  234.1 7.4 %conditional.6 = (bf16[8,32,2048]{2,1,0:T(8,128)(2,1)S(1)}, bf16[8,32,2048]{2,1,0:T(8,128)(2,1)}, f32[8,32,2048]{2,1,0:T(8,128)}, bf16[8,32,2048]{2,1,0:T(8,128)(2,1)S(1)}, bf16[32,2048]{1,0:T(8,128)(2,1)S(1)}) conditional(s32[]{:T(128)} %convert_element_type.149, (bf16[8,32,2048]{2,1,0:T(8,128)(2,1)S(1)}, bf16[8,32,2048]{2,1,0:T(8,128)(2,1)}, ...), branch_computations={%region_1.1_spmd, %region_2.3_spmd} | conditional | flops 269877280 | bytes 10372557 | solution.py:106
  235.2 5.6 bitcast_dynamic-update-slice_fusion.1
  241.5 4.4 collective-permute-start
  249.5 11.7 %collective-permute-start = (bf16[32,2048]{1,0:T(8,128)(2,1)S(1)}, bf16[32,2048]{1,0:T(8,128)(2,1)S(1)}, u32[]{:S(2)}, u32[]{:S(2)}) collective-permute-start(bf16[32,2048]{1,0:T(8,128)(2,1)S(1)} %get-tuple-element.722), channel_id=1, source_target_pairs={{0,16},{1,17},{2,18},{3,19},{4,20},{5,21},{6,22},{7,23},{8,24},{9,... | collective-permute-start | bytes 393224 | tf_op jit(solution)/shard_map/while/body/eval_jaxpr/ppermute | solution.py:14
  266.8 162.1 %while.37 = (s32[]{:T(128)}, bf16[32,2048]{1,0:T(8,128)(2,1)S(1)}, bf16[8,32,2048]{2,1,0:T(8,128)(2,1)}, bf16[8,32,2048]{2,1,0:T(8,128)(2,1)S(1)}, f32[2048]{0:T...) while((s32[]{:T(128)}, bf16[32,2048]{1,0:T(8,128)(2,1)S(1)}, ...), condition=%wide.region_17.18_spmd, body=%wide.region_11.17_spmd.sunk | while | flops 271122464 | bytes 11324200 | solution.py:183
  269.4 19.5 %collective-permute-done.1 = bf16[32,2048]{1,0:T(8,128)(2,1)S(1)} collective-permute-done((bf16[32,2048]{1,0:T(8,128)(2,1)S(1)}, bf16[32,2048]{1,0:T(8,128)(2,1)S(1)}, u32[]{:S(2)}, u32[]{:S(2)}) %collective-permute-start.1) | collective-permute-done | bytes 131104 | tf_op jit(solution)/shard_map/while/body/eval_jaxpr/ppermute | solution.py:14
  290.2 9.2 %conditional.7 = (bf16[8,32,2048]{2,1,0:T(8,128)(2,1)}, bf16[8,32,2048]{2,1,0:T(8,128)(2,1)S(1)}, f32[2048]{0:T(1024)S(1)}, bf16[32,2048]{1,0:T(8,128)(2,1)S(1)}) conditional(s32[]{:T(128)} %convert_element_type.150, (bf16[8,32,2048]{2,1,0:T(8,128)(2,1)}, bf16[8,32,2048]{2,1,0:T(8,128)(2,1)S(1)}, f32[2048]{0:T(1024)S(1)}) %tuple.103, (pred[]{:T(512)}, ...), branch_computations={%region_12.12_spmd, %region_13.16_spmd} | conditional | flops 271122464 | bytes 10799561 | solution.py:178
  292.2 6.1 fusion.21
  300.7 5.6 collective-permute-done.1
  307.5 9.2 %conditional.7 = (bf16[8,32,2048]{2,1,0:T(8,128)(2,1)}, bf16[8,32,2048]{2,1,0:T(8,128)(2,1)S(1)}, f32[2048]{0:T(1024)S(1)}, bf16[32,2048]{1,0:T(8,128)(2,1)S(1)}) conditional(s32[]{:T(128)} %convert_element_type.150, (bf16[8,32,2048]{2,1,0:T(8,128)(2,1)}, bf16[8,32,2048]{2,1,0:T(8,128)(2,1)S(1)}, f32[2048]{0:T(1024)S(1)}) %tuple.103, (pred[]{:T(512)}, ...), branch_computations={%region_12.12_spmd, %region_13.16_spmd} | conditional | flops 271122464 | bytes 10799561 | solution.py:178
  309.5 6.1 fusion.21
  317.9 5.6 collective-permute-done.1
  324.7 9.2 %conditional.7 = (bf16[8,32,2048]{2,1,0:T(8,128)(2,1)}, bf16[8,32,2048]{2,1,0:T(8,128)(2,1)S(1)}, f32[2048]{0:T(1024)S(1)}, bf16[32,2048]{1,0:T(8,128)(2,1)S(1)}) conditional(s32[]{:T(128)} %convert_element_type.150, (bf16[8,32,2048]{2,1,0:T(8,128)(2,1)}, bf16[8,32,2048]{2,1,0:T(8,128)(2,1)S(1)}, f32[2048]{0:T(1024)S(1)}) %tuple.103, (pred[]{:T(512)}, ...), branch_computations={%region_12.12_spmd, %region_13.16_spmd} | conditional | flops 271122464 | bytes 10799561 | solution.py:178
  326.8 6.1 fusion.21
  335.2 5.6 collective-permute-done.1
  342.0 9.2 %conditional.7 = (bf16[8,32,2048]{2,1,0:T(8,128)(2,1)}, bf16[8,32,2048]{2,1,0:T(8,128)(2,1)S(1)}, f32[2048]{0:T(1024)S(1)}, bf16[32,2048]{1,0:T(8,128)(2,1)S(1)}) conditional(s32[]{:T(128)} %convert_element_type.150, (bf16[8,32,2048]{2,1,0:T(8,128)(2,1)}, bf16[8,32,2048]{2,1,0:T(8,128)(2,1)S(1)}, f32[2048]{0:T(1024)S(1)}) %tuple.103, (pred[]{:T(512)}, ...), branch_computations={%region_12.12_spmd, %region_13.16_spmd} | conditional | flops 271122464 | bytes 10799561 | solution.py:178
  344.1 6.1 fusion.21
  352.5 5.6 collective-permute-done.1
  359.3 9.2 %conditional.7 = (bf16[8,32,2048]{2,1,0:T(8,128)(2,1)}, bf16[8,32,2048]{2,1,0:T(8,128)(2,1)S(1)}, f32[2048]{0:T(1024)S(1)}, bf16[32,2048]{1,0:T(8,128)(2,1)S(1)}) conditional(s32[]{:T(128)} %convert_element_type.150, (bf16[8,32,2048]{2,1,0:T(8,128)(2,1)}, bf16[8,32,2048]{2,1,0:T(8,128)(2,1)S(1)}, f32[2048]{0:T(1024)S(1)}) %tuple.103, (pred[]{:T(512)}, ...), branch_computations={%region_12.12_spmd, %region_13.16_spmd} | conditional | flops 271122464 | bytes 10799561 | solution.py:178
  361.4 6.1 fusion.21
  369.8 6.5 collective-permute-done.1
  377.5 9.2 %conditional.7 = (bf16[8,32,2048]{2,1,0:T(8,128)(2,1)}, bf16[8,32,2048]{2,1,0:T(8,128)(2,1)S(1)}, f32[2048]{0:T(1024)S(1)}, bf16[32,2048]{1,0:T(8,128)(2,1)S(1)}) conditional(s32[]{:T(128)} %convert_element_type.150, (bf16[8,32,2048]{2,1,0:T(8,128)(2,1)}, bf16[8,32,2048]{2,1,0:T(8,128)(2,1)S(1)}, f32[2048]{0:T(1024)S(1)}) %tuple.103, (pred[]{:T(512)}, ...), branch_computations={%region_12.12_spmd, %region_13.16_spmd} | conditional | flops 271122464 | bytes 10799561 | solution.py:178
  379.6 6.1 fusion.21
  388.0 6.3 collective-permute-done.1
  395.6 9.2 %conditional.7 = (bf16[8,32,2048]{2,1,0:T(8,128)(2,1)}, bf16[8,32,2048]{2,1,0:T(8,128)(2,1)S(1)}, f32[2048]{0:T(1024)S(1)}, bf16[32,2048]{1,0:T(8,128)(2,1)S(1)}) conditional(s32[]{:T(128)} %convert_element_type.150, (bf16[8,32,2048]{2,1,0:T(8,128)(2,1)}, bf16[8,32,2048]{2,1,0:T(8,128)(2,1)S(1)}, f32[2048]{0:T(1024)S(1)}) %tuple.103, (pred[]{:T(512)}, ...), branch_computations={%region_12.12_spmd, %region_13.16_spmd} | conditional | flops 271122464 | bytes 10799561 | solution.py:178
  397.6 6.1 fusion.21
  406.1 5.6 collective-permute-done.1
  412.9 9.2 %conditional.7 = (bf16[8,32,2048]{2,1,0:T(8,128)(2,1)}, bf16[8,32,2048]{2,1,0:T(8,128)(2,1)S(1)}, f32[2048]{0:T(1024)S(1)}, bf16[32,2048]{1,0:T(8,128)(2,1)S(1)}) conditional(s32[]{:T(128)} %convert_element_type.150, (bf16[8,32,2048]{2,1,0:T(8,128)(2,1)}, bf16[8,32,2048]{2,1,0:T(8,128)(2,1)S(1)}, f32[2048]{0:T(1024)S(1)}) %tuple.103, (pred[]{:T(512)}, ...), branch_computations={%region_12.12_spmd, %region_13.16_spmd} | conditional | flops 271122464 | bytes 10799561 | solution.py:178
  414.9 6.1 fusion.21
  423.3 5.6 collective-permute-done.1
  428.9 7.5 %bitcast_convert_fusion = bf16[2048,2048]{1,0:T(8,128)(2,1)} fusion(bf16[8,32,2048]{2,1,0:T(8,128)(2,1)} %get-tuple-element.491, bf16[8,32,2048]{2,1,0:T(8,128)(2,1)} %get-tuple-element.496), kind=kOutput, calls=%fused_computation.61 | convolution fusion | flops 2151677952 | bytes 10485760 | tf_op jit(solution)/shard_map/dot_general | solution.py:190
  440.2 39.2 %psum.15 = f32[2048]{0:T(1024)} all-reduce(f32[2048]{0:T(1024)S(1)} %get-tuple-element.500), channel_id=1, replica_groups=mesh['section'=2,'rep'=4,'sub'=4] {'section','rep','sub'}, use_global_device_ids=true, to_apply=%region_21.22 | all-reduce | flops 2048 | bytes 16384 | tf_op jit(solution)/shard_map/psum | solution.py:198
  479.5 29.2 %psum.14 = f32[1,2048]{1,0:T(1,128)} all-reduce(f32[1,2048]{1,0:T(1,128)S(1)} %bitcast.88), channel_id=1, replica_groups=mesh['section'=2,'rep'=4,'sub'=4] {'rep','sub'}, use_global_device_ids=true, to_apply=%region_19.20 | all-reduce | flops 2048 | bytes 16384 | tf_op jit(solution)/shard_map/psum | solution.py:197
  508.7 30.6 %reduce-scatter.3.cloned.1.call-done = bf16[128,2048]{1,0:T(8,128)(2,1)} async-done(((bf16[2048,2048]{1,0:T(8,128)(2,1)}), bf16[128,2048]{1,0:T(8,128)(2,1)}) %reduce-scatter.3.cloned.1.call-update) | async-done | bytes 524304 | tf_op jit(solution)/shard_map/reduce_scatter | solution.py:189
  541.4 128.7 %reduce-scatter.5.cloned.1.call-done = f32[8,2048]{1,0:T(8,128)} async-done(((f32[256,2048]{1,0:T(8,128)}), f32[8,2048]{1,0:T(8,128)}) %reduce-scatter.5.cloned.1.call-update) | async-done | bytes 65552 | tf_op jit(solution)/shard_map/reduce_scatter | solution.py:206
  (149 shorter events, 87.2 us)
Async XLA Ops:
  7.2 41.0 %all-gather.3.cloned.1.call-start = ((), (), s32[]{:S(2)}) async-start(), calls=%async_computation.2 | async-start | bytes 1114112 | tf_op jit(solution)/shard_map/all_gather | solution.py:67
  7.9 116.5 %all-gather.5.cloned.1.call-start = ((), (), s32[]{:S(2)}) async-start(), calls=%async_computation.3 | async-start | bytes 8912896 | tf_op jit(solution)/shard_map/all_gather | solution.py:68
  8.6 530.6 %reduce-scatter.3.cloned.1.call-start = ((), (), s32[]{:S(2)}) async-start(), calls=%async_computation.4 | async-start | bytes 8912896 | tf_op jit(solution)/shard_map/reduce_scatter | solution.py:189
  125.9 1.4 copy-start.2
  127.3 136.4 %copy-start.6 = (f32[2048]{0:T(1024)S(1)}, f32[2048]{0:T(1024)}, u32[]{:S(2)}) copy-start(f32[2048]{0:T(1024)} %param.21) | copy-start | bytes 24580
  127.3 136.4 %copy-start.7 = (s32[8,32]{1,0:T(8,128)S(1)}, s32[8,32]{1,0:T(8,128)}, u32[]{:S(2)}) copy-start(s32[8,32]{1,0:T(8,128)} %param.17) | copy-start | bytes 3076
  135.9 4.7 collective-permute-start
  149.1 7.0 %collective-permute-start = (bf16[32,2048]{1,0:T(8,128)(2,1)S(1)}, bf16[32,2048]{1,0:T(8,128)(2,1)S(1)}, u32[]{:S(2)}, u32[]{:S(2)}) collective-permute-start(bf16[32,2048]{1,0:T(8,128)(2,1)S(1)} %get-tuple-element.722), channel_id=1, source_target_pairs={{0,16},{1,17},{2,18},{3,19},{4,20},{5,21},{6,22},{7,23},{8,24},{9,... | collective-permute-start | bytes 393224 | tf_op jit(solution)/shard_map/while/body/eval_jaxpr/ppermute | solution.py:14
  164.6 6.9 %collective-permute-start = (bf16[32,2048]{1,0:T(8,128)(2,1)S(1)}, bf16[32,2048]{1,0:T(8,128)(2,1)S(1)}, u32[]{:S(2)}, u32[]{:S(2)}) collective-permute-start(bf16[32,2048]{1,0:T(8,128)(2,1)S(1)} %get-tuple-element.722), channel_id=1, source_target_pairs={{0,16},{1,17},{2,18},{3,19},{4,20},{5,21},{6,22},{7,23},{8,24},{9,... | collective-permute-start | bytes 393224 | tf_op jit(solution)/shard_map/while/body/eval_jaxpr/ppermute | solution.py:14
  180.0 6.9 %collective-permute-start = (bf16[32,2048]{1,0:T(8,128)(2,1)S(1)}, bf16[32,2048]{1,0:T(8,128)(2,1)S(1)}, u32[]{:S(2)}, u32[]{:S(2)}) collective-permute-start(bf16[32,2048]{1,0:T(8,128)(2,1)S(1)} %get-tuple-element.722), channel_id=1, source_target_pairs={{0,16},{1,17},{2,18},{3,19},{4,20},{5,21},{6,22},{7,23},{8,24},{9,... | collective-permute-start | bytes 393224 | tf_op jit(solution)/shard_map/while/body/eval_jaxpr/ppermute | solution.py:14
  195.4 6.9 %collective-permute-start = (bf16[32,2048]{1,0:T(8,128)(2,1)S(1)}, bf16[32,2048]{1,0:T(8,128)(2,1)S(1)}, u32[]{:S(2)}, u32[]{:S(2)}) collective-permute-start(bf16[32,2048]{1,0:T(8,128)(2,1)S(1)} %get-tuple-element.722), channel_id=1, source_target_pairs={{0,16},{1,17},{2,18},{3,19},{4,20},{5,21},{6,22},{7,23},{8,24},{9,... | collective-permute-start | bytes 393224 | tf_op jit(solution)/shard_map/while/body/eval_jaxpr/ppermute | solution.py:14
  210.7 6.8 %collective-permute-start = (bf16[32,2048]{1,0:T(8,128)(2,1)S(1)}, bf16[32,2048]{1,0:T(8,128)(2,1)S(1)}, u32[]{:S(2)}, u32[]{:S(2)}) collective-permute-start(bf16[32,2048]{1,0:T(8,128)(2,1)S(1)} %get-tuple-element.722), channel_id=1, source_target_pairs={{0,16},{1,17},{2,18},{3,19},{4,20},{5,21},{6,22},{7,23},{8,24},{9,... | collective-permute-start | bytes 393224 | tf_op jit(solution)/shard_map/while/body/eval_jaxpr/ppermute | solution.py:14
  226.1 6.9 %collective-permute-start = (bf16[32,2048]{1,0:T(8,128)(2,1)S(1)}, bf16[32,2048]{1,0:T(8,128)(2,1)S(1)}, u32[]{:S(2)}, u32[]{:S(2)}) collective-permute-start(bf16[32,2048]{1,0:T(8,128)(2,1)S(1)} %get-tuple-element.722), channel_id=1, source_target_pairs={{0,16},{1,17},{2,18},{3,19},{4,20},{5,21},{6,22},{7,23},{8,24},{9,... | collective-permute-start | bytes 393224 | tf_op jit(solution)/shard_map/while/body/eval_jaxpr/ppermute | solution.py:14
  241.5 6.9 %collective-permute-start = (bf16[32,2048]{1,0:T(8,128)(2,1)S(1)}, bf16[32,2048]{1,0:T(8,128)(2,1)S(1)}, u32[]{:S(2)}, u32[]{:S(2)}) collective-permute-start(bf16[32,2048]{1,0:T(8,128)(2,1)S(1)} %get-tuple-element.722), channel_id=1, source_target_pairs={{0,16},{1,17},{2,18},{3,19},{4,20},{5,21},{6,22},{7,23},{8,24},{9,... | collective-permute-start | bytes 393224 | tf_op jit(solution)/shard_map/while/body/eval_jaxpr/ppermute | solution.py:14
  249.5 14.2 %collective-permute-start = (bf16[32,2048]{1,0:T(8,128)(2,1)S(1)}, bf16[32,2048]{1,0:T(8,128)(2,1)S(1)}, u32[]{:S(2)}, u32[]{:S(2)}) collective-permute-start(bf16[32,2048]{1,0:T(8,128)(2,1)S(1)} %get-tuple-element.722), channel_id=1, source_target_pairs={{0,16},{1,17},{2,18},{3,19},{4,20},{5,21},{6,22},{7,23},{8,24},{9,... | collective-permute-start | bytes 393224 | tf_op jit(solution)/shard_map/while/body/eval_jaxpr/ppermute | solution.py:14
  265.0 1.6 copy-start
  268.1 20.8 %collective-permute-start.1 = (bf16[32,2048]{1,0:T(8,128)(2,1)S(1)}, bf16[32,2048]{1,0:T(8,128)(2,1)S(1)}, u32[]{:S(2)}, u32[]{:S(2)}) collective-permute-start(bf16[32,2048]{1,0:T(8,128)(2,1)S(1)} %get-tuple-element.740), channel_id=1, source_target_pairs={{16,0},{17,1},{18,2},{19,3},{20,4},{21,5},{22,6},{23,7},{24,8},{25... | collective-permute-start | bytes 393224 | tf_op jit(solution)/shard_map/while/body/eval_jaxpr/ppermute | solution.py:14
  299.3 6.9 %collective-permute-start.1 = (bf16[32,2048]{1,0:T(8,128)(2,1)S(1)}, bf16[32,2048]{1,0:T(8,128)(2,1)S(1)}, u32[]{:S(2)}, u32[]{:S(2)}) collective-permute-start(bf16[32,2048]{1,0:T(8,128)(2,1)S(1)} %get-tuple-element.740), channel_id=1, source_target_pairs={{16,0},{17,1},{18,2},{19,3},{20,4},{21,5},{22,6},{23,7},{24,8},{25... | collective-permute-start | bytes 393224 | tf_op jit(solution)/shard_map/while/body/eval_jaxpr/ppermute | solution.py:14
  316.6 6.9 %collective-permute-start.1 = (bf16[32,2048]{1,0:T(8,128)(2,1)S(1)}, bf16[32,2048]{1,0:T(8,128)(2,1)S(1)}, u32[]{:S(2)}, u32[]{:S(2)}) collective-permute-start(bf16[32,2048]{1,0:T(8,128)(2,1)S(1)} %get-tuple-element.740), channel_id=1, source_target_pairs={{16,0},{17,1},{18,2},{19,3},{20,4},{21,5},{22,6},{23,7},{24,8},{25... | collective-permute-start | bytes 393224 | tf_op jit(solution)/shard_map/while/body/eval_jaxpr/ppermute | solution.py:14
  333.9 6.9 %collective-permute-start.1 = (bf16[32,2048]{1,0:T(8,128)(2,1)S(1)}, bf16[32,2048]{1,0:T(8,128)(2,1)S(1)}, u32[]{:S(2)}, u32[]{:S(2)}) collective-permute-start(bf16[32,2048]{1,0:T(8,128)(2,1)S(1)} %get-tuple-element.740), channel_id=1, source_target_pairs={{16,0},{17,1},{18,2},{19,3},{20,4},{21,5},{22,6},{23,7},{24,8},{25... | collective-permute-start | bytes 393224 | tf_op jit(solution)/shard_map/while/body/eval_jaxpr/ppermute | solution.py:14
  351.2 6.9 %collective-permute-start.1 = (bf16[32,2048]{1,0:T(8,128)(2,1)S(1)}, bf16[32,2048]{1,0:T(8,128)(2,1)S(1)}, u32[]{:S(2)}, u32[]{:S(2)}) collective-permute-start(bf16[32,2048]{1,0:T(8,128)(2,1)S(1)} %get-tuple-element.740), channel_id=1, source_target_pairs={{16,0},{17,1},{18,2},{19,3},{20,4},{21,5},{22,6},{23,7},{24,8},{25... | collective-permute-start | bytes 393224 | tf_op jit(solution)/shard_map/while/body/eval_jaxpr/ppermute | solution.py:14
  368.5 7.8 %collective-permute-start.1 = (bf16[32,2048]{1,0:T(8,128)(2,1)S(1)}, bf16[32,2048]{1,0:T(8,128)(2,1)S(1)}, u32[]{:S(2)}, u32[]{:S(2)}) collective-permute-start(bf16[32,2048]{1,0:T(8,128)(2,1)S(1)} %get-tuple-element.740), channel_id=1, source_target_pairs={{16,0},{17,1},{18,2},{19,3},{20,4},{21,5},{22,6},{23,7},{24,8},{25... | collective-permute-start | bytes 393224 | tf_op jit(solution)/shard_map/while/body/eval_jaxpr/ppermute | solution.py:14
  386.7 7.6 %collective-permute-start.1 = (bf16[32,2048]{1,0:T(8,128)(2,1)S(1)}, bf16[32,2048]{1,0:T(8,128)(2,1)S(1)}, u32[]{:S(2)}, u32[]{:S(2)}) collective-permute-start(bf16[32,2048]{1,0:T(8,128)(2,1)S(1)} %get-tuple-element.740), channel_id=1, source_target_pairs={{16,0},{17,1},{18,2},{19,3},{20,4},{21,5},{22,6},{23,7},{24,8},{25... | collective-permute-start | bytes 393224 | tf_op jit(solution)/shard_map/while/body/eval_jaxpr/ppermute | solution.py:14
  404.8 6.9 %collective-permute-start.1 = (bf16[32,2048]{1,0:T(8,128)(2,1)S(1)}, bf16[32,2048]{1,0:T(8,128)(2,1)S(1)}, u32[]{:S(2)}, u32[]{:S(2)}) collective-permute-start(bf16[32,2048]{1,0:T(8,128)(2,1)S(1)} %get-tuple-element.740), channel_id=1, source_target_pairs={{16,0},{17,1},{18,2},{19,3},{20,4},{21,5},{22,6},{23,7},{24,8},{25... | collective-permute-start | bytes 393224 | tf_op jit(solution)/shard_map/while/body/eval_jaxpr/ppermute | solution.py:14
  422.0 6.9 %collective-permute-start.1 = (bf16[32,2048]{1,0:T(8,128)(2,1)S(1)}, bf16[32,2048]{1,0:T(8,128)(2,1)S(1)}, u32[]{:S(2)}, u32[]{:S(2)}) collective-permute-start(bf16[32,2048]{1,0:T(8,128)(2,1)S(1)} %get-tuple-element.740), channel_id=1, source_target_pairs={{16,0},{17,1},{18,2},{19,3},{20,4},{21,5},{22,6},{23,7},{24,8},{25... | collective-permute-start | bytes 393224 | tf_op jit(solution)/shard_map/while/body/eval_jaxpr/ppermute | solution.py:14
  428.9 7.5 %copy-start.4 = (bf16[8,32,2048]{2,1,0:T(8,128)(2,1)}, bf16[8,32,2048]{2,1,0:T(8,128)(2,1)S(1)}, u32[]{:S(2)}) copy-start(bf16[8,32,2048]{2,1,0:T(8,128)(2,1)S(1)} %get-tuple-element.498) | copy-start | bytes 3145732
  436.4 1.6 copy-start.1
  436.4 1.9 copy-start.5
  436.5 233.6 %reduce-scatter.5.cloned.1.call-start = ((), (), s32[]{:S(2)}) async-start(), calls=%async_computation.5 | async-start | bytes 2162688 | tf_op jit(solution)/shard_map/reduce_scatter | solution.py:206
Sparse Core Ops, SparseCore 0:
  10.1 37.9 all-gather.2
  50.3 74.0 all-gather.4
  436.6 102.6 reduce-scatter.2
  541.9 128.0 reduce-scatter.4
where the time goes:
time: 690 us; the launch traced here: 677 us
  waiting for transfers between devices  362 us (52%)
  matrix products  106 us (15%)
  blocking collectives  68.4 us (10%)
  starting transfers between devices  55.3 us (8%)
  other arithmetic  34.9 us (5%)
  local copies, waits for them, and re-layouts  24.5 us (4%)
  between operations  13.9 us (2%)
  loops' own time  12 us (2%)
    reduce_scatter x1, waiting for transfers between devices, body(): lax.psum_scatter(contribution, ('section', 'rep', 'sub'), scatter_dimensi...  129 us
    ppermute x18, waiting for transfers between devices, passed_along(): lax.ppermute(value, axis, [(source, source + steps) for source in range(i...  89.1 us
    all_gather x1, waiting for transfers between devices, body(): lax.all_gather(section_weight, ('rep', 'sub'), axis=1, tiled=True)[0]  73.6 us
    ppermute x18, starting transfers between devices, passed_along(): lax.ppermute(value, axis, [(source, source + steps) for source in range(i...  55.1 us
    dot_general x8, matrix products, backward_compute(): lax.dot_general(grad_pre, weight, contract_last, preferred_element_type=j...  48.8 us
    dot_general x8, matrix products, forward_compute(): pre_act = jnp.dot(rounded, weight, preferred_element_type=jnp.float32)  44.7 us
    psum x1, blocking collectives, body(): final_total = lax.psum(final_part, ('section', 'rep', 'sub'))  39.2 us
    all_gather x1, waiting for transfers between devices, body(): vocab_table = lax.all_gather(embedding, ('rep', 'sub'), axis=0, tiled=True)  38.7 us
  transfers between devices with their start and end apart: 22, of which 22 were waited for; matrix products, arithmetic and copies ran while one was open for 1% of the time, Pallas kernels for 0%

commit v1 on v0

--- a/solution.py
+++ b/solution.py
@@ -53,7 +53,7 @@
     return lax.dynamic_update_index_in_dim(buffer, update, slot_index, 0)
 
 
-def body(token_ids, target_ids, embedding, section_weight, section_gain, final_gain):
+def pipeline_body(token_ids, target_ids, embedding, section_weight, section_gain, final_gain):
     sections = lax.axis_size("section")
     position = lax.axis_index("section")
     micro_count = token_ids.shape[0]
@@ -209,6 +209,85 @@
     return (weight_part[None], gain_total[None], embed_total, final_total)
 
 
+def fits_replicated(mesh, weight_shape):
+    layers, rows, columns = weight_shape
+    return layers * rows * columns * 2 <= 16 * 1024 * 1024
+
+
+def replicated_body(token_ids, target_ids, embedding, section_weight, section_gain, final_gain):
+    axes = ("section", "rep", "sub")
+    sections = lax.axis_size("section")
+    position = lax.axis_index("section")
+    features = embedding.shape[1]
+    vocab_rows = embedding.shape[0] * lax.axis_size(("rep", "sub"))
+    token_count = token_ids.size // sections
+    contract_last = (((1,), (1,)), ((), ()))
+    contract_first = (((0,), (0,)), ((), ()))
+    vocab_table = lax.all_gather(embedding, ("rep", "sub"), axis=0, tiled=True)
+    weights = lax.all_gather(section_weight[0], axes, axis=0, tiled=True)
+    weights = weights.reshape(sections, features, features)
+    gains = lax.all_gather(section_gain, "section", axis=0, tiled=True)
+    my_tokens = lax.dynamic_slice_in_dim(token_ids.reshape(-1), position * token_count, token_count)
+    my_targets = lax.dynamic_slice_in_dim(target_ids.reshape(-1), position * token_count, token_count)
+    vocab_iota = jnp.arange(vocab_rows, dtype=jnp.int32)
+    onehot_in = (my_tokens[:, None] == vocab_iota[None, :]).astype(jnp.bfloat16)
+    residual = jnp.dot(onehot_in, vocab_table, preferred_element_type=jnp.float32).astype(
+        jnp.bfloat16
+    )
+    saved = []
+    for layer in range(sections):
+        normed, scale_inv, rounded = normalize(residual, gains[layer])
+        pre_act = jnp.dot(rounded, weights[layer], preferred_element_type=jnp.float32)
+        saved.append((normed, scale_inv, rounded, pre_act))
+        residual = (residual.astype(jnp.float32) + gelu(pre_act)).astype(jnp.bfloat16)
+    logit_scale = float(features) ** (-0.5)
+    normed, scale_inv, final_rows = normalize(residual, final_gain)
+    logits = (
+        lax.dot_general(final_rows, vocab_table, contract_last, preferred_element_type=jnp.float32)
+        * logit_scale
+    )
+    exp_logit = jnp.exp(logits)
+    probability = exp_logit / jnp.sum(exp_logit, axis=-1, keepdims=True)
+    onehot_out = (my_targets[:, None] == vocab_iota[None, :]).astype(jnp.float32)
+    grad_logit = ((probability - onehot_out) * logit_scale).astype(jnp.bfloat16)
+    embed_head = lax.dot_general(
+        grad_logit, final_rows, contract_first, preferred_element_type=jnp.float32
+    )
+    grad_final = jnp.dot(grad_logit, vocab_table, preferred_element_type=jnp.float32)
+    grad_in, final_part = norm_back(grad_final, normed, scale_inv, final_gain)
+    grad_residual = grad_in.astype(jnp.bfloat16)
+    weight_parts = []
+    small_parts = [final_part]
+    for layer in reversed(range(sections)):
+        normed, scale_inv, rounded, pre_act = saved[layer]
+        grad_float = grad_residual.astype(jnp.float32)
+        grad_pre = (grad_float * gelu_slope(pre_act)).astype(jnp.bfloat16)
+        weight_parts.append(
+            lax.dot_general(
+                rounded, grad_pre, contract_first, preferred_element_type=jnp.float32
+            ).astype(jnp.bfloat16)
+        )
+        grad_norm = lax.dot_general(
+            grad_pre, weights[layer], contract_last, preferred_element_type=jnp.float32
+        )
+        grad_in, gain_part = norm_back(grad_norm, normed, scale_inv, gains[layer])
+        small_parts.append(gain_part)
+        grad_residual = (grad_float + grad_in).astype(jnp.bfloat16)
+    embed_part = embed_head + lax.dot_general(
+        onehot_in, grad_residual, contract_first, preferred_element_type=jnp.float32
+    )
+    return finish(weight_parts[::-1], embed_part, jnp.stack(small_parts), axes, position, sections)
+
+
+def finish(weight_parts, embed_part, small_part, axes, position, sections):
+    weight_all = jnp.concatenate(weight_parts, axis=0)
+    weight_total = lax.psum_scatter(weight_all, axes, scatter_dimension=0, tiled=True)
+    embed_total = lax.psum_scatter(embed_part, axes, scatter_dimension=0, tiled=True)
+    small_total = lax.psum(small_part, axes)
+    gain_total = lax.dynamic_slice_in_dim(small_total, sections - position, 1, axis=0)
+    return (weight_total.astype(jnp.float32)[None], gain_total, embed_total, small_total[0])
+
+
 def solution(mesh):
     in_specs = (
         P(None, ("rep", "sub")),
@@ -224,4 +303,13 @@
         P(("section", "rep", "sub"), None),
         P(),
     )
-    return jax.shard_map(body, mesh=mesh, in_specs=in_specs, out_specs=out_specs, check_vma=False)
+
+    def step(*arguments):
+        tokens = arguments[0].size // (mesh.shape["rep"] * mesh.shape["sub"])
+        replicated = fits_replicated(mesh, arguments[3].shape) and tokens % mesh.shape["section"] == 0
+        chosen = replicated_body if replicated else pipeline_body
+        return jax.shard_map(
+            chosen, mesh=mesh, in_specs=in_specs, out_specs=out_specs, check_vma=False
+        )(*arguments)
+
+    return step

time: 690 us -> 530 us (0.77)
  the two profiles are of different devices: /device:TPU:8 before, /device:TPU:0 now
where the time goes in v1:
time: 530 us; the launch traced here: 529 us
  waiting for transfers between devices  417 us (79%)
  blocking collectives  52.3 us (10%)
  matrix products  32.6 us (6%)
  between operations  13.9 us (3%)
  other arithmetic  10.3 us (2%)
    reduce_scatter x1, waiting for transfers between devices, finish(): lax.psum_scatter(embed_part, axes, scatter_dimension=0, tiled=True)  140 us
    reduce_scatter x1, waiting for transfers between devices, finish(): lax.psum_scatter(weight_all, axes, scatter_dimension=0, tiled=True)  127 us
    all_gather x1, waiting for transfers between devices, replicated_body(): weights = lax.all_gather(section_weight[0], axes, axis=0, tiled=True)  115 us
    psum x1, blocking collectives, finish(): small_total = lax.psum(small_part, axes)  46.7 us
    all_gather x1, waiting for transfers between devices, replicated_body(): vocab_table = lax.all_gather(embedding, ('rep', 'sub'), axis=0, tiled=True)  34.8 us
    dot_general x2, matrix products, replicated_body(): lax.dot_general(grad_pre, weights[layer], contract_last, preferred_elemen...  12.7 us
  transfers between devices with their start and end apart: 4, of which 4 were waited for; matrix products, arithmetic and copies ran while one was open for 3% of the time, Pallas kernels for 0%

profile of v1, /device:TPU:0, one launch (start us, length us, event | category | flops | bytes accessed | tf_op | source)
XLA Modules:
  0.0 529.2 jit_solution(16493197933310688039)
XLA Ops:
  7.2 0.0 all-gather.5.cloned.1.call-start
  7.2 0.7 all-gather.5.cloned.1.call-update
  7.9 0.0 all-gather.7.cloned.1.call-start
  7.9 0.7 all-gather.7.cloned.1.call-update
  8.6 0.0 reduce-scatter.3.cloned.1.call-start
  8.7 0.8 reshape.59
  9.5 0.8 reshape.60
  10.2 0.1 dynamic_slice.9
  10.3 0.1 dynamic_slice.10
  10.4 5.6 %all-gather.1 = f32[2,1,2048]{2,1,0:T(1,128)S(1)} all-gather(f32[1,1,2048]{2,1,0:T(1,128)} %bitcast.37), channel_id=1, replica_groups=mesh['section'=2,'rep'=4,'sub'=4] {'section'}, dimensions={0}, use_global_device_ids=true | all-gather | bytes 24576 | tf_op jit(solution)/shard_map/all_gather | solution.py:229
  16.0 34.8 %all-gather.5.cloned.1.call-done = bf16[256,2048]{1,0:T(8,128)(2,1)} async-done(((bf16[16,2048]{1,0:T(8,128)(2,1)}), bf16[256,2048]{1,0:T(8,128)(2,1)}) %all-gather.5.cloned.1.call-update) | async-done | bytes 1048592 | tf_op jit(solution)/shard_map/all_gather | solution.py:226
  50.7 1.7 multiply_reduce_fusion.2
  52.4 114.5 %all-gather.7.cloned.1.call-done = bf16[1,4096,2048]{2,1,0:T(8,128)(2,1)} async-done(((bf16[1,128,2048]{2,1,0:T(8,128)(2,1)}), bf16[1,4096,2048]{2,1,0:T(8,128)(2,1)}) %all-gather.7.cloned.1.call-update) | async-done | bytes 16777232 | tf_op jit(solution)/shard_map/all_gather | solution.py:227
  166.9 4.5 fusion.32
  171.4 0.0 copy-start
  171.4 0.0 copy-start.1
  171.5 4.6 fusion.20
  176.1 0.0 copy-done
  176.1 0.0 copy-done.1
  176.1 0.6 fusion.59
  176.7 0.5 fusion.19
  177.2 2.8 convolution_convert_fusion
  180.1 6.8 %fusion.31 = (f32[2048]{0:T(1024)S(1)}, f32[128]{0:T(128)S(1)}, f32[128,2048]{1,0:T(8,128)S(1)}) fusion(bf16[128,2048]{1,0:T(8,128)(2,1)S(1)} %get-tuple-element.13, f32[128]{0:T(128)S(1)} %add_rsqrt_fusion.1, f32[2048]{0:T(1024)S(1)} %bitcast.35, bf16[1,4096,2048]{2,1,0:T(8,128)(2,1)} %all-gather.7.cloned.1.call-done, ...), kind=kOutput, calls=%fused_computation.52 | convolution fusion | flops 1082652544 | bytes 12609536 | tf_op jit(solution)/shard_map/dot_general | solution.py:270
  186.9 0.6 fusion.22
  187.5 2.6 convolution_convert_fusion.1
  190.1 7.5 %pad_maximum_fusion = bf16[4096,2048]{1,0:T(8,128)(2,1)} fusion(bf16[2048,2048]{1,0:T(8,128)(2,1)S(1)} %convolution_convert_fusion, bf16[2048,2048]{1,0:T(8,128)(2,1)S(1)} %convolution_convert_fusion.1), kind=kLoop, calls=%fused_computation | loop fusion | flops 33554432 | bytes 33554432 | tf_op jit(solution)/shard_map/concatenate | solution.py:283
  197.6 0.0 reduce-scatter.3.cloned.1.call-update
  197.6 0.2 reduce-scatter.5.cloned.1.call-start
  197.8 5.9 %multiply_reduce_fusion = (f32[128]{0:T(128)S(1)}, f32[2048]{0:T(1024)S(1)}, f32[128,2048]{1,0:T(8,128)S(1)}) fusion(f32[128,2048]{1,0:T(8,128)S(1)} %get-tuple-element.19, f32[2048]{0:T(1024)S(1)} %bitcast.31, f32[128]{0:T(128)S(1)} %add_rsqrt_fusion.2, bf16[1,4096,2048]{2,1,0:T(8,128)(2,1)} %all-gather.7.cloned.1.call-done, ...), kind=kOutput, calls=%fused_computation.63 | convolution fusion | flops 1080555392 | bytes 12076032 | tf_op jit(solution)/shard_map/dot_general | solution.py:270
  203.7 0.6 fusion.48
  204.3 2.0 convolution_add_fusion
  206.3 0.0 reduce-scatter.5.cloned.1.call-update
  206.3 46.7 %psum.7 = f32[3,2048]{1,0:T(4,128)S(1)} all-reduce(f32[3,2048]{1,0:T(4,128)S(1)} %pad_maximum_fusion.1), channel_id=1, replica_groups=mesh['section'=2,'rep'=4,'sub'=4] {'section','rep','sub'}, use_global_device_ids=true, to_apply=%region_10.0 | all-reduce | flops 6144 | bytes 49152 | tf_op jit(solution)/shard_map/psum | solution.py:286
  253.1 0.6 fusion.57
  253.7 126.5 %reduce-scatter.3.cloned.1.call-done = bf16[128,2048]{1,0:T(8,128)(2,1)} async-done(((bf16[4096,2048]{1,0:T(8,128)(2,1)}), bf16[128,2048]{1,0:T(8,128)(2,1)}) %reduce-scatter.3.cloned.1.call-update) | async-done | bytes 524304 | tf_op jit(solution)/shard_map/reduce_scatter | solution.py:284
  380.3 2.1 bitcast_convert_fusion
  382.4 140.3 %reduce-scatter.5.cloned.1.call-done = f32[8,2048]{1,0:T(8,128)} async-done(((f32[256,2048]{1,0:T(8,128)}), f32[8,2048]{1,0:T(8,128)}) %reduce-scatter.5.cloned.1.call-update) | async-done | bytes 65552 | tf_op jit(solution)/shard_map/reduce_scatter | solution.py:285
  (8 shorter events, 0.1 us)
Async XLA Ops:
  7.2 43.6 %all-gather.5.cloned.1.call-start = ((), (), s32[]{:S(2)}) async-start(), calls=%async_computation.2 | async-start | bytes 1114112 | tf_op jit(solution)/shard_map/all_gather | solution.py:226
  7.9 159.0 %all-gather.7.cloned.1.call-start = ((), (), s32[]{:S(2)}) async-start(), calls=%async_computation.5 | async-start | bytes 17301504 | tf_op jit(solution)/shard_map/all_gather | solution.py:227
  8.6 371.6 %reduce-scatter.3.cloned.1.call-start = ((), (), s32[]{:S(2)}) async-start(), calls=%async_computation.3 | async-start | bytes 17301504 | tf_op jit(solution)/shard_map/reduce_scatter | solution.py:284
  171.4 4.7 copy-start
  171.4 4.7 copy-start.1
  197.6 325.0 %reduce-scatter.5.cloned.1.call-start = ((), (), s32[]{:S(2)}) async-start(), calls=%async_computation.4 | async-start | bytes 2162688 | tf_op jit(solution)/shard_map/reduce_scatter | solution.py:285
Sparse Core Ops, SparseCore 0:
  10.1 40.5 all-gather.4
  53.6 113.3 all-gather.6
  197.7 182.4 reduce-scatter.2
  382.9 139.6 reduce-scatter.4

commit v2 on v1

--- a/solution.py
+++ b/solution.py
@@ -1,6 +1,9 @@
+import functools
 import jax
 import jax.numpy as jnp
 from jax import lax
+from jax.experimental import pallas as pl
+from jax.experimental.pallas import tpu as pltpu
 from jax.sharding import PartitionSpec as P
 
 epsilon = 1e-06
@@ -209,6 +212,260 @@
     return (weight_part[None], gain_total[None], embed_total, final_total)
 
 
+row_step = 16
+
+
+def add_rows(target, other, columns=None):
+    @pl.loop(0, target.shape[0] // row_step)
+    def _(step):
+        rows = pl.ds(pl.multiple_of(step * row_step, row_step), row_step)
+        extra = other[rows, :] if columns is None else other[rows, columns]
+        target[rows, :] = (target[rows, :].astype(jnp.float32) + extra.astype(jnp.float32)).astype(
+            target.dtype
+        )
+
+
+def scatter_kernel(
+    reps, weight_ref, embed_ref, small_ref, weight_out, embed_out, small_out, *scratch
+):
+    position, rep, sub = (lax.axis_index(name) for name in ("section", "rep", "sub"))
+    chip, core = sub // 2, sub % 2
+    partner = {"section": position, "rep": rep, "sub": chip * 2 + 1 - core}
+    across_y = {"section": 1 - position, "rep": rep, "sub": sub}
+    across_x = {"section": position, "rep": rep, "sub": (1 - chip) * 2 + core}
+    up = {"section": position, "rep": lax.rem(rep + 1, reps), "sub": sub}
+    down = {"section": position, "rep": lax.rem(rep + reps - 1, reps), "sub": sub}
+    small_sum, small_in, send_sem, recv_sem = scratch[-4:]
+    tensors = []
+    for index, (source, output) in enumerate(((weight_ref, weight_out), (embed_ref, embed_out))):
+        tensors.append((source, output) + tuple(scratch[7 * index : 7 * index + 7]))
+
+    barrier = pltpu.get_barrier_semaphore()
+    others = [partner, across_y, across_x] + [
+        {"section": position, "rep": lax.rem(rep + hop, reps), "sub": sub}
+        for hop in range(1, reps)
+    ]
+    for other in others:
+        pl.semaphore_signal(barrier, inc=1, device_id=other, device_id_type=pl.DeviceIdType.MESH)
+    pl.semaphore_wait(barrier, len(others))
+
+    counter = [0]
+
+    def message(source, target, device):
+        number = counter[0]
+        counter[0] += 1
+        return pltpu.make_async_remote_copy(
+            src_ref=source,
+            dst_ref=target,
+            send_sem=send_sem.at[number],
+            recv_sem=recv_sem.at[number],
+            device_id=device,
+            device_id_type=pl.DeviceIdType.MESH,
+        )
+
+    pending = []
+
+    def launch(copy):
+        copy.start()
+        pending.append(copy)
+        return copy
+
+    rep_order = []
+    for near in range((reps + 1) // 2):
+        for far in (reps - 1 - near, near):
+            if far not in rep_order:
+                rep_order.append(far)
+    kinds = ((1, 1), (1, 0), (0, 1), (0, 0))
+
+    def towards(flip, own):
+        return 1 - own if flip else own
+
+    small_sum[0] = small_ref[...]
+    small_copies = [launch(message(small_sum.at[0], small_in.at[0], partner))]
+
+    core_copies = {}
+    for flip_s, flip_x in kinds:
+        for r in rep_order:
+            for t, tensor in enumerate(tensors):
+                s, x = towards(flip_s, position), towards(flip_x, chip)
+                core_copies[flip_s, flip_x, r, t] = launch(
+                    message(tensor[0].at[s, r, x, 1 - core], tensor[2].at[s, r, x], partner)
+                )
+    first_a, first_b = {}, {}
+    for flip_s, flip_x in kinds:
+        s, x = towards(flip_s, position), towards(flip_x, chip)
+        for r in rep_order:
+            for t, tensor in enumerate(tensors):
+                source, output, held, y_a, x_a, x_b, y_b = tensor[:7]
+                core_copies[flip_s, flip_x, r, t].wait_recv()
+                add_rows(held.at[s, r, x], source.at[s, r, x, core])
+                half = held.shape[-1] // 2
+                if flip_s:
+                    first_a[flip_x, r, t] = launch(
+                        message(held.at[s, r, x, :, pl.ds(0, half)], y_a.at[x, r], across_y)
+                    )
+                if flip_x:
+                    first_b[flip_s, r, t] = launch(
+                        message(held.at[s, r, x, :, pl.ds(half, half)], x_b.at[s, r], across_x)
+                    )
+    small_copies[0].wait_recv()
+    small_sum[1] = small_sum[0] + small_in[0]
+    small_copies.append(launch(message(small_sum.at[1], small_in.at[1], across_y)))
+
+    second_a, second_b = {}, {}
+    for flip in (1, 0):
+        for r in rep_order:
+            for t, tensor in enumerate(tensors):
+                source, output, held, y_a, x_a, x_b, y_b = tensor[:7]
+                half = held.shape[-1] // 2
+                x = towards(flip, chip)
+                first_a[flip, r, t].wait_recv()
+                add_rows(y_a.at[x, r], held.at[position, r, x], pl.ds(0, half))
+                s = towards(flip, position)
+                first_b[flip, r, t].wait_recv()
+                add_rows(x_b.at[s, r], held.at[s, r, chip], pl.ds(half, half))
+                if flip:
+                    second_a[r, t] = launch(message(y_a.at[x, r], x_a.at[r], across_x))
+                    second_b[r, t] = launch(message(x_b.at[s, r], y_b.at[r], across_y))
+    small_copies[1].wait_recv()
+    small_sum[2] = small_sum[1] + small_in[1]
+    small_copies.append(launch(message(small_sum.at[2], small_in.at[2], across_x)))
+
+    for r in rep_order:
+        for t, tensor in enumerate(tensors):
+            source, output, held, y_a, x_a, x_b, y_b = tensor[:7]
+            second_a[r, t].wait_recv()
+            add_rows(x_a.at[r], y_a.at[chip, r])
+            second_b[r, t].wait_recv()
+            add_rows(y_b.at[r], x_b.at[position, r])
+    small_copies[2].wait_recv()
+    small_sum[3] = small_sum[2] + small_in[2]
+    small_gather = []
+    for hop in range(1, reps):
+        there = {"section": position, "rep": lax.rem(rep + hop, reps), "sub": sub}
+        small_gather.append(launch(message(small_sum.at[3], small_in.at[2 + hop], there)))
+
+    ends = []
+    for step in range(reps - 1):
+        for t, tensor in enumerate(tensors):
+            x_a, y_b = tensor[4], tensor[6]
+            z_up, z_down = tensor[7:9]
+            for color, own in enumerate((x_a, y_b)):
+                for buffer, target, device, upward in (
+                    (z_up, reps - 1 - step, up, True),
+                    (z_down, step, down, False),
+                ):
+                    at_start = rep == (0 if upward else reps - 1)
+                    passes = rep < target if upward else rep > target
+                    here = buffer.at[color, target]
+                    fresh = message(own.at[target], here, device)
+                    counter[0] -= 1
+                    passed = message(here, here, device)
+
+                    @pl.when(jnp.logical_and(jnp.logical_not(at_start), jnp.logical_or(passes, rep == target)))
+                    def _():
+                        passed.wait_recv()
+
+                    @pl.when(jnp.logical_and(jnp.logical_not(at_start), passes))
+                    def _():
+                        add_rows(here, own.at[target])
+                        passed.start()
+
+                    @pl.when(jnp.logical_and(at_start, passes))
+                    def _():
+                        fresh.start()
+
+                    ends.append((passes, passed))
+    for t, tensor in enumerate(tensors):
+        output, x_a, y_b = tensor[1], tensor[4], tensor[6]
+        z_up, z_down = tensor[7:9]
+        half = x_a.shape[-1]
+        for color, own in enumerate((x_a, y_b)):
+
+            @pl.loop(0, own.shape[1] // row_step)
+            def _(step):
+                rows = pl.ds(pl.multiple_of(step * row_step, row_step), row_step)
+                output[rows, pl.ds(color * half, half)] = own[rep, rows, :].astype(jnp.float32)
+
+            for buffer, edge in ((z_up, 0), (z_down, reps - 1)):
+
+                @pl.when(rep != edge)
+                def _():
+                    @pl.loop(0, own.shape[1] // row_step)
+                    def _(step):
+                        rows = pl.ds(pl.multiple_of(step * row_step, row_step), row_step)
+                        output[rows, pl.ds(color * half, half)] += buffer[color, rep, rows, :].astype(
+                            jnp.float32
+                        )
+
+    for copy in small_gather:
+        copy.wait_recv()
+    total = small_sum[3]
+    for hop in range(1, reps):
+        total = total + small_in[2 + hop]
+    small_out[...] = total
+    for copy in pending:
+        copy.wait_send()
+    for passes, copy in ends:
+
+        @pl.when(passes)
+        def _():
+            copy.wait_send()
+
+
+def scatter_sums(weight_part, embed_part, small_part):
+    sections, reps, subs = (lax.axis_size(name) for name in ("section", "rep", "sub"))
+    devices = sections * reps * subs
+    kinds = (sections, reps, subs // 2, 2)
+    weight_rows = weight_part.shape[0] // devices
+    columns = weight_part.shape[1]
+    embed_rows = embed_part.shape[0] // devices
+    fold = max(1, row_step // embed_rows)
+    weight_in = weight_part.reshape(kinds + (weight_rows, columns))
+    embed_in = embed_part.astype(jnp.bfloat16).reshape(
+        kinds + (embed_rows * fold, columns // fold)
+    )
+    pad = (-small_part.shape[0]) % 8
+    small_in = jnp.pad(small_part, ((0, pad), (0, 0)))
+    scratch = []
+    for rows, width in (weight_in.shape[-2:], embed_in.shape[-2:]):
+        half = width // 2
+        for lead in (
+            (sections, reps, subs // 2, rows, width),
+            (subs // 2, reps, rows, half),
+            (reps, rows, half),
+            (sections, reps, rows, half),
+            (reps, rows, half),
+            (2, reps, rows, half),
+            (2, reps, rows, half),
+        ):
+            scratch.append(pltpu.VMEM(lead, jnp.bfloat16))
+    messages = 2 * (4 * reps + 4 * reps + 2 * reps + 4 * (reps - 1)) + 2 * 4 * reps + 3 + reps
+    scratch += [
+        pltpu.VMEM((4,) + small_in.shape, jnp.float32),
+        pltpu.VMEM((2 + reps,) + small_in.shape, jnp.float32),
+        pltpu.SemaphoreType.DMA((messages,)),
+        pltpu.SemaphoreType.DMA((messages,)),
+    ]
+    vmem = pl.BlockSpec(memory_space=pltpu.VMEM)
+    weight_sum, embed_sum, small_sum = pl.pallas_call(
+        functools.partial(scatter_kernel, reps),
+        out_shape=(
+            jax.ShapeDtypeStruct(weight_in.shape[-2:], jnp.float32),
+            jax.ShapeDtypeStruct(embed_in.shape[-2:], jnp.float32),
+            jax.ShapeDtypeStruct(small_in.shape, jnp.float32),
+        ),
+        in_specs=[vmem] * 3,
+        out_specs=(vmem,) * 3,
+        scratch_shapes=scratch,
+        compiler_params=pltpu.CompilerParams(
+            collective_id=1, has_side_effects=True, vmem_limit_bytes=60 * 1024 * 1024
+        ),
+        name="scatter_sums",
+    )(weight_in, embed_in, small_in)
+    return weight_sum, embed_sum.reshape(embed_rows, columns), small_sum[: small_part.shape[0]]
+
+
 def fits_replicated(mesh, weight_shape):
     layers, rows, columns = weight_shape
     return layers * rows * columns * 2 <= 16 * 1024 * 1024
@@ -281,6 +538,10 @@
 
 def finish(weight_parts, embed_part, small_part, axes, position, sections):
     weight_all = jnp.concatenate(weight_parts, axis=0)
+    if sections == 2 and lax.axis_size("sub") == 4 and lax.axis_size("rep") > 1:
+        weight_total, embed_total, small_total = scatter_sums(weight_all, embed_part, small_part)
+        gain_total = lax.dynamic_slice_in_dim(small_total, sections - position, 1, axis=0)
+        return (weight_total[None], gain_total, embed_total, small_total[0])
     weight_total = lax.psum_scatter(weight_all, axes, scatter_dimension=0, tiled=True)
     embed_total = lax.psum_scatter(embed_part, axes, scatter_dimension=0, tiled=True)
     small_total = lax.psum(small_part, axes)

time: 530 us -> 464 us (0.88)
  the two profiles are of different devices: /device:TPU:0 before, /device:TPU:8 now
where the time goes in v2:
time: 464 us
  Pallas kernels  236 us (51%)
  waiting for transfers between devices  149 us (32%)
  matrix products  35.5 us (8%)
  other arithmetic  15 us (3%)
  between operations  14.2 us (3%)
  local copies, waits for them, and re-layouts  9.55 us (2%)
    pallas_call x1, Pallas kernels, scatter_sums(): pl.pallas_call(functools.partial(scatter_kernel, reps), out_shape=(jax.Sh...  236 us
    all_gather x1, waiting for transfers between devices, replicated_body(): weights = lax.all_gather(section_weight[0], axes, axis=0, tiled=True)  115 us
    all_gather x1, waiting for transfers between devices, replicated_body(): vocab_table = lax.all_gather(embedding, ('rep', 'sub'), axis=0, tiled=True)  33.3 us
    concatenate x1, other arithmetic, finish(): weight_all = jnp.concatenate(weight_parts, axis=0)  13.7 us
    dot_general x2, matrix products, replicated_body(): lax.dot_general(rounded, grad_pre, contract_first, preferred_element_type...  11.8 us
    dot_general x2, matrix products, replicated_body(): lax.dot_general(grad_pre, weights[layer], contract_last, preferred_elemen...  10.3 us
    dot_general x2, matrix products, replicated_body(): jnp.dot(rounded, weights[layer], preferred_element_type=jnp.float32)  9.31 us
  transfers between devices with their start and end apart: 2, of which 2 were waited for; matrix products, arithmetic and copies ran while one was open for 1% of the time, Pallas kernels for 0%

profile of v2, /device:TPU:8, one launch (start us, length us, event | category | flops | bytes accessed | tf_op | source)
XLA Modules:
  0.0 463.7 jit_solution(1542252400780253593)
XLA Ops:
  7.2 0.0 all-gather.5.cloned.1.call-start
  7.2 0.7 all-gather.5.cloned.1.call-update
  7.9 0.0 all-gather.7.cloned.1.call-start
  7.9 0.7 all-gather.7.cloned.1.call-update
  8.7 0.8 reshape.68
  9.4 0.8 reshape.69
  10.2 0.1 dynamic_slice.9
  10.3 0.1 dynamic_slice.10
  10.3 4.6 all-gather.1
  14.9 33.3 %all-gather.5.cloned.1.call-done = bf16[256,2048]{1,0:T(8,128)(2,1)} async-done(((bf16[16,2048]{1,0:T(8,128)(2,1)}), bf16[256,2048]{1,0:T(8,128)(2,1)}) %all-gather.5.cloned.1.call-update) | async-done | bytes 1048592 | tf_op jit(solution)/shard_map/all_gather | solution.py:483
  48.2 1.7 multiply_reduce_fusion.2
  49.8 114.7 %all-gather.7.cloned.1.call-done = bf16[1,4096,2048]{2,1,0:T(8,128)(2,1)} async-done(((bf16[1,128,2048]{2,1,0:T(8,128)(2,1)}), bf16[1,4096,2048]{2,1,0:T(8,128)(2,1)}) %all-gather.7.cloned.1.call-update) | async-done | bytes 16777232 | tf_op jit(solution)/shard_map/all_gather | solution.py:484
  164.5 4.5 fusion.33
  169.1 0.0 copy-start
  169.1 0.0 copy-start.1
  169.1 4.8 %fusion.21 = (f32[128]{0:T(128)S(1)}, bf16[128,2048]{1,0:T(8,128)(2,1)S(1)}, f32[128,2048]{1,0:T(8,128)S(1)}) fusion(bf16[128,2048]{1,0:T(8,128)(2,1)S(1)} %get-tuple-element.19, bf16[1,4096,2048]{2,1,0:T(8,128)(2,1)} %all-gather.7.cloned.1.call-done, f32[2048]{0:T(1024)S(1)} %bitcast.34, f32[128]{0:T(128)S(1)} %add_rsqrt_fusion.1), kind=kOutput, calls=%fused_computation.42 | convolution fusion | flops 1078460288 | bytes 11019264 | tf_op jit(solution)/shard_map/dot_general | solution.py:497
  173.9 0.0 copy-done
  173.9 0.0 copy-done.1
  173.9 0.6 fusion.59
  174.5 0.6 fusion.49
  175.0 0.5 fusion.20
  175.6 6.0 %convolution_convert_fusion = bf16[2048,2048]{1,0:T(8,128)(2,1)} fusion(bf16[128,2048]{1,0:T(8,128)(2,1)S(1)} %get-tuple-element.19, f32[2048]{0:T(1024)S(1)} %bitcast.35, f32[128]{0:T(128)S(1)} %add_rsqrt_fusion.1, f32[128,2048]{1,0:T(8,128)S(1)} %get-tuple-element.25, bf16[128,2048]{1,0:T(8,128)(2,1)S(1)} %get-tuple-element.17, ...), kind=kOutput, calls=%fused_computation.3 | convolution fusion | flops 1086062592 | bytes 11552256 | tf_op jit(solution)/shard_map/dot_general | solution.py:523
  181.6 0.0 slice-start
  181.6 0.0 slice-start.1
  181.6 0.0 slice-start.2
  181.6 6.9 %fusion.32 = (f32[2048]{0:T(1024)S(1)}, f32[128]{0:T(128)S(1)}, f32[128,2048]{1,0:T(8,128)S(1)}) fusion(bf16[128,2048]{1,0:T(8,128)(2,1)S(1)} %get-tuple-element.19, f32[128]{0:T(128)S(1)} %add_rsqrt_fusion.1, f32[2048]{0:T(1024)S(1)} %bitcast.36, bf16[1,4096,2048]{2,1,0:T(8,128)(2,1)} %all-gather.7.cloned.1.call-done, ...), kind=kOutput, calls=%fused_computation.53 | convolution fusion | flops 1082652544 | bytes 12609536 | tf_op jit(solution)/shard_map/dot_general | solution.py:527
  188.6 0.5 fusion.23
  189.1 0.0 slice-start.3
  189.1 5.8 %convolution_convert_fusion.1 = bf16[2048,2048]{1,0:T(8,128)(2,1)} fusion(f32[128,2048]{1,0:T(8,128)S(1)} %get-tuple-element.23, f32[2048]{0:T(1024)S(1)} %bitcast.31, f32[128]{0:T(128)S(1)} %add_rsqrt_fusion.2, bf16[128,2048]{1,0:T(8,128)(2,1)S(1)} %fusion.23, f32[128,2048]{1,0:T(8,128)S(1)} %get-tuple-element.24), kind=kOutput, calls=%fused_computation.4 | convolution fusion | flops 1083965440 | bytes 11018752 | tf_op jit(solution)/shard_map/dot_general | solution.py:523
  194.9 0.0 slice-done
  194.9 0.0 slice-done.1
  194.9 0.0 slice-done.2
  194.9 0.0 slice-done.3
  194.9 3.4 multiply_reduce_fusion
  198.4 0.6 fusion.4
  199.0 1.2 reshape.71.embed_ref
  200.2 13.7 %pad_maximum_fusion = bf16[4096,2048]{1,0:T(8,128)(2,1)} fusion(bf16[2048,2048]{1,0:T(8,128)(2,1)} %convolution_convert_fusion, bf16[2048,2048]{1,0:T(8,128)(2,1)} %convolution_convert_fusion.1), kind=kLoop, calls=%fused_computation | loop fusion | flops 33554432 | bytes 33554432 | tf_op jit(solution)/shard_map/concatenate | solution.py:540
  213.9 0.7 select_maximum_fusion.small_ref
  214.6 235.6 %scatter_sums.1 = (f32[128,2048]{1,0:T(8,128)}, f32[16,1024]{1,0:T(8,128)}, f32[8,2048]{1,0:T(8,128)}) custom-call(bf16[2,4,2,2,128,2048]{5,4,3,2,1,0:T(8,128)(2,1)} %bitcast.28, bf16[2,4,2,2,16,1024]{5,4,3,2,1,0:T(8,128)(2,1)} %reshape.71.embed_ref, f32[8,2048]{1,0:T(8,128)} %select_maximum_fusion.small_ref), custom_call_target="tpu_custom_call" | custom-call | tf_op jit(solution)/shard_map/scatter_sums/pallas_call | solution.py:451
  450.2 1.4 slice.30
  451.6 0.8 slice.29
  452.5 1.5 reshape.72
  454.0 0.6 constant_dynamic-slice_fusion
  454.6 2.3 copy.11
  (8 shorter events, 0.0 us)
Async XLA Ops:
  7.2 41.0 %all-gather.5.cloned.1.call-start = ((), (), s32[]{:S(2)}) async-start(), calls=%async_computation | async-start | bytes 1114112 | tf_op jit(solution)/shard_map/all_gather | solution.py:483
  7.9 156.6 %all-gather.7.cloned.1.call-start = ((), (), s32[]{:S(2)}) async-start(), calls=%async_computation.1 | async-start | bytes 17301504 | tf_op jit(solution)/shard_map/all_gather | solution.py:484
  169.1 4.8 %copy-start = (bf16[256,2048]{1,0:T(8,128)(2,1)S(1)}, bf16[256,2048]{1,0:T(8,128)(2,1)}, u32[]{:S(2)}) copy-start(bf16[256,2048]{1,0:T(8,128)(2,1)} %all-gather.5.cloned.1.call-done) | copy-start | bytes 3145732
  169.1 4.8 %copy-start.1 = (f32[2048]{0:T(1024)S(1)}, f32[2048]{0:T(1024)}, u32[]{:S(2)}) copy-start(f32[2048]{0:T(1024)} %param.11) | copy-start | bytes 24580
  181.6 13.3 %slice-start = ((s8[16777216]{0:T(1024)(128)(4,1)}), s8[4194304]{0:T(1024)(128)(4,1)S(1)}, s32[]{:S(2)}) async-start(s8[16777216]{0:T(1024)(128)(4,1)} %bitcast.43), calls=%async_computation.2 | async-start | bytes 8388608
  181.6 13.3 %slice-start.1 = ((s8[16777216]{0:T(1024)(128)(4,1)}), s8[4194304]{0:T(1024)(128)(4,1)S(1)}, s32[]{:S(2)}) async-start(s8[16777216]{0:T(1024)(128)(4,1)} %bitcast.43), calls=%async_computation.3 | async-start | bytes 8388608
  181.6 13.3 %slice-start.2 = ((s8[16777216]{0:T(1024)(128)(4,1)}), s8[4194304]{0:T(1024)(128)(4,1)S(1)}, s32[]{:S(2)}) async-start(s8[16777216]{0:T(1024)(128)(4,1)} %bitcast.43), calls=%async_computation.4 | async-start | bytes 8388608
  189.1 5.8 %slice-start.3 = ((s8[16777216]{0:T(1024)(128)(4,1)}), s8[4194304]{0:T(1024)(128)(4,1)S(1)}, s32[]{:S(2)}) async-start(s8[16777216]{0:T(1024)(128)(4,1)} %bitcast.43), calls=%async_computation.5 | async-start | bytes 8388608
Sparse Core Ops, SparseCore 0:
  10.1 37.9 all-gather.4
  51.0 113.4 all-gather.6

commit v3 on v2

--- a/solution.py
+++ b/solution.py
@@ -480,7 +480,14 @@
     token_count = token_ids.size // sections
     contract_last = (((1,), (1,)), ((), ()))
     contract_first = (((0,), (0,)), ((), ()))
-    vocab_table = lax.all_gather(embedding, ("rep", "sub"), axis=0, tiled=True)
+    half = features // 2
+    vocab_table = jnp.concatenate(
+        [
+            lax.all_gather(part, ("rep", "sub"), axis=0, tiled=True)
+            for part in (embedding[:, :half], embedding[:, half:])
+        ],
+        axis=1,
+    )
     weights = lax.all_gather(section_weight[0], axes, axis=0, tiled=True)
     weights = weights.reshape(sections, features, features)
     gains = lax.all_gather(section_gain, "section", axis=0, tiled=True)

time: 464 us -> 430 us (0.927)
  waiting for transfers between devices: 149 us -> 71.8 us
  blocking collectives: 4.56 us -> 48.4 us
    all_gather x0 -> x2, blocking collectives: none -> 43.9 us  [replicated_body(): lax.all_gather(part, ('rep', 'sub'), axis=0, tiled=True)]
    all_gather x1, waiting for transfers between devices: 115 us -> 71.1 us  [replicated_body(): weights = lax.all_gather(section_weight[0], axes, axis=0, tiled=True)]
    all_gather x1 -> x0, waiting for transfers between devices: 33.3 us -> none  [replicated_body(): vocab_table = lax.all_gather(embedding, ('rep', 'sub'), axis=0, tiled=True)]
  transfers between devices with their start and end apart: 2 -> 1, of which waited for: 2 -> 1; matrix products, arithmetic and copies ran while one was open for 1% -> 1% of each run, Pallas kernels for 0% -> 0%
where the time goes in v3:
time: 430 us
  Pallas kernels  236 us (55%)
  waiting for transfers between devices  71.8 us (17%)
  blocking collectives  48.4 us (11%)
  matrix products  34.2 us (8%)
  other arithmetic  15 us (3%)
  between operations  14.2 us (3%)
  local copies, waits for them, and re-layouts  10.4 us (2%)
    pallas_call x1, Pallas kernels, scatter_sums(): pl.pallas_call(functools.partial(scatter_kernel, reps), out_shape=(jax.Sh...  236 us
    all_gather x1, waiting for transfers between devices, replicated_body(): weights = lax.all_gather(section_weight[0], axes, axis=0, tiled=True)  71.1 us
    all_gather x2, blocking collectives, replicated_body(): lax.all_gather(part, ('rep', 'sub'), axis=0, tiled=True)  43.9 us
    concatenate x1, other arithmetic, finish(): weight_all = jnp.concatenate(weight_parts, axis=0)  13.7 us
    dot_general x2, matrix products, replicated_body(): lax.dot_general(rounded, grad_pre, contract_first, preferred_element_type...  11.8 us
    dot_general x2, matrix products, replicated_body(): lax.dot_general(grad_pre, weights[layer], contract_last, preferred_elemen...  10.3 us
    dot_general x2, matrix products, replicated_body(): jnp.dot(rounded, weights[layer], preferred_element_type=jnp.float32)  9.27 us
  transfers between devices with their start and end apart: 1, of which 1 were waited for; matrix products, arithmetic and copies ran while one was open for 1% of the time, Pallas kernels for 0%

profile of v3, /device:TPU:8, one launch (start us, length us, event | category | flops | bytes accessed | tf_op | source)
XLA Modules:
  0.0 429.6 jit_solution(9889521058361049683)
XLA Ops:
  7.2 0.0 all-gather.4.cloned.1.call-start
  7.2 0.7 all-gather.4.cloned.1.call-update
  7.9 0.8 reshape.68
  8.7 0.8 reshape.69
  9.4 0.1 dynamic_slice.9
  9.5 0.1 dynamic_slice.10
  9.6 4.6 %all-gather.1 = f32[2,1,2048]{2,1,0:T(1,128)S(1)} all-gather(f32[1,1,2048]{2,1,0:T(1,128)} %bitcast.38), channel_id=1, replica_groups=mesh['section'=2,'rep'=4,'sub'=4] {'section'}, dimensions={0}, use_global_device_ids=true | all-gather | bytes 24576 | tf_op jit(solution)/shard_map/all_gather | solution.py:493
  14.1 0.8 fusion.58
  14.9 21.8 %all_gather.12 = bf16[256,1024]{1,0:T(8,128)(2,1)S(1)} all-gather(bf16[16,1024]{1,0:T(8,128)(2,1)S(1)} %get-tuple-element.21), channel_id=1, replica_groups=mesh['section'=2,'rep'=4,'sub'=4] {'rep','sub'}, dimensions={0}, use_global_device_ids=true | all-gather | bytes 557056 | tf_op jit(solution)/shard_map/all_gather | solution.py:486
  36.7 22.1 %all_gather.13 = bf16[256,1024]{1,0:T(8,128)(2,1)S(1)} all-gather(bf16[16,1024]{1,0:T(8,128)(2,1)S(1)} %get-tuple-element.20), channel_id=1, replica_groups=mesh['section'=2,'rep'=4,'sub'=4] {'rep','sub'}, dimensions={0}, use_global_device_ids=true | all-gather | bytes 557056 | tf_op jit(solution)/shard_map/all_gather | solution.py:486
  58.9 0.4 multiply_reduce_fusion.2
  59.3 71.1 %all-gather.4.cloned.1.call-done = bf16[1,4096,2048]{2,1,0:T(8,128)(2,1)} async-done(((bf16[1,128,2048]{2,1,0:T(8,128)(2,1)}), bf16[1,4096,2048]{2,1,0:T(8,128)(2,1)}) %all-gather.4.cloned.1.call-update) | async-done | bytes 16777232 | tf_op jit(solution)/shard_map/all_gather | solution.py:491
  130.4 4.6 %fusion.33 = (f32[128]{0:T(128)S(1)}, bf16[128,2048]{1,0:T(8,128)(2,1)S(1)}, f32[128,2048]{1,0:T(8,128)S(1)}) fusion(f32[128,2048]{1,0:T(8,128)S(1)} %get-tuple-element.25, bf16[1,4096,2048]{2,1,0:T(8,128)(2,1)} %all-gather.4.cloned.1.call-done, f32[2048]{0:T(1024)S(1)} %bitcast.30, f32[128]{0:T(128)S(1)} %add_rsqrt_fusion.2), kind=kOutput, calls=%fused_computation.54 | convolution fusion | flops 1077936000 | bytes 12067840 | tf_op jit(solution)/shard_map/dot_general | solution.py:504
  135.0 0.0 copy-start
  135.0 4.7 %fusion.21 = (f32[128]{0:T(128)S(1)}, bf16[128,2048]{1,0:T(8,128)(2,1)S(1)}, f32[128,2048]{1,0:T(8,128)S(1)}) fusion(bf16[128,2048]{1,0:T(8,128)(2,1)S(1)} %get-tuple-element.19, bf16[1,4096,2048]{2,1,0:T(8,128)(2,1)} %all-gather.4.cloned.1.call-done, f32[2048]{0:T(1024)S(1)} %bitcast.34, f32[128]{0:T(128)S(1)} %add_rsqrt_fusion.1), kind=kOutput, calls=%fused_computation.42 | convolution fusion | flops 1078460288 | bytes 11019264 | tf_op jit(solution)/shard_map/dot_general | solution.py:504
  139.8 0.0 copy-done
  139.8 0.6 fusion.60
  140.3 0.6 fusion.20
  140.9 0.6 fusion.49
  141.5 6.0 %convolution_convert_fusion = bf16[2048,2048]{1,0:T(8,128)(2,1)} fusion(bf16[128,2048]{1,0:T(8,128)(2,1)S(1)} %get-tuple-element.19, f32[2048]{0:T(1024)S(1)} %bitcast.35, f32[128]{0:T(128)S(1)} %add_rsqrt_fusion.1, f32[128,2048]{1,0:T(8,128)S(1)} %get-tuple-element.27, bf16[128,2048]{1,0:T(8,128)(2,1)S(1)} %get-tuple-element.17, ...), kind=kOutput, calls=%fused_computation.3 | convolution fusion | flops 1086062592 | bytes 11552256 | tf_op jit(solution)/shard_map/dot_general | solution.py:530
  147.5 0.0 slice-start
  147.5 0.0 slice-start.1
  147.5 0.0 slice-start.2
  147.5 6.9 %fusion.32 = (f32[2048]{0:T(1024)S(1)}, f32[128]{0:T(128)S(1)}, f32[128,2048]{1,0:T(8,128)S(1)}) fusion(bf16[128,2048]{1,0:T(8,128)(2,1)S(1)} %get-tuple-element.19, f32[128]{0:T(128)S(1)} %add_rsqrt_fusion.1, f32[2048]{0:T(1024)S(1)} %bitcast.36, bf16[1,4096,2048]{2,1,0:T(8,128)(2,1)} %all-gather.4.cloned.1.call-done, ...), kind=kOutput, calls=%fused_computation.53 | convolution fusion | flops 1082652544 | bytes 12609536 | tf_op jit(solution)/shard_map/dot_general | solution.py:534
  154.5 0.5 fusion.23
  155.0 0.0 slice-start.3
  155.0 5.8 %convolution_convert_fusion.1 = bf16[2048,2048]{1,0:T(8,128)(2,1)} fusion(f32[128,2048]{1,0:T(8,128)S(1)} %get-tuple-element.25, f32[2048]{0:T(1024)S(1)} %bitcast.31, f32[128]{0:T(128)S(1)} %add_rsqrt_fusion.2, bf16[128,2048]{1,0:T(8,128)(2,1)S(1)} %fusion.23, f32[128,2048]{1,0:T(8,128)S(1)} %get-tuple-element.26), kind=kOutput, calls=%fused_computation.4 | convolution fusion | flops 1083965440 | bytes 11018752 | tf_op jit(solution)/shard_map/dot_general | solution.py:530
  160.8 0.0 slice-done
  160.8 0.0 slice-done.1
  160.8 0.0 slice-done.2
  160.8 0.0 slice-done.3
  160.8 3.4 multiply_reduce_fusion
  164.2 0.7 fusion.4
  164.9 1.2 reshape.71.embed_ref
  166.1 13.7 %pad_maximum_fusion = bf16[4096,2048]{1,0:T(8,128)(2,1)} fusion(bf16[2048,2048]{1,0:T(8,128)(2,1)} %convolution_convert_fusion, bf16[2048,2048]{1,0:T(8,128)(2,1)} %convolution_convert_fusion.1), kind=kLoop, calls=%fused_computation | loop fusion | flops 33554432 | bytes 33554432 | tf_op jit(solution)/shard_map/concatenate | solution.py:547
  179.8 0.7 select_maximum_fusion.small_ref
  180.5 235.6 %scatter_sums.1 = (f32[128,2048]{1,0:T(8,128)}, f32[16,1024]{1,0:T(8,128)}, f32[8,2048]{1,0:T(8,128)}) custom-call(bf16[2,4,2,2,128,2048]{5,4,3,2,1,0:T(8,128)(2,1)} %bitcast.28, bf16[2,4,2,2,16,1024]{5,4,3,2,1,0:T(8,128)(2,1)} %reshape.71.embed_ref, f32[8,2048]{1,0:T(8,128)} %select_maximum_fusion.small_ref), custom_call_target="tpu_custom_call" | custom-call | tf_op jit(solution)/shard_map/scatter_sums/pallas_call | solution.py:451
  416.1 1.4 slice.38
  417.5 0.8 slice.37
  418.4 1.5 reshape.72
  419.9 0.6 constant_dynamic-slice_fusion
  420.5 2.3 copy.12
  (10 shorter events, 0.1 us)
Async XLA Ops:
  7.2 123.3 %all-gather.4.cloned.1.call-start = ((), (), s32[]{:S(2)}) async-start(), calls=%async_computation | async-start | bytes 17301504 | tf_op jit(solution)/shard_map/all_gather | solution.py:491
  135.0 4.8 %copy-start = (f32[2048]{0:T(1024)S(1)}, f32[2048]{0:T(1024)}, u32[]{:S(2)}) copy-start(f32[2048]{0:T(1024)} %param.11) | copy-start | bytes 24580
  147.5 13.3 %slice-start = ((s8[16777216]{0:T(1024)(128)(4,1)}), s8[4194304]{0:T(1024)(128)(4,1)S(1)}, s32[]{:S(2)}) async-start(s8[16777216]{0:T(1024)(128)(4,1)} %bitcast.43), calls=%async_computation.1 | async-start | bytes 8388608
  147.5 13.3 %slice-start.1 = ((s8[16777216]{0:T(1024)(128)(4,1)}), s8[4194304]{0:T(1024)(128)(4,1)S(1)}, s32[]{:S(2)}) async-start(s8[16777216]{0:T(1024)(128)(4,1)} %bitcast.43), calls=%async_computation.2 | async-start | bytes 8388608
  147.5 13.3 %slice-start.2 = ((s8[16777216]{0:T(1024)(128)(4,1)}), s8[4194304]{0:T(1024)(128)(4,1)S(1)}, s32[]{:S(2)}) async-start(s8[16777216]{0:T(1024)(128)(4,1)} %bitcast.43), calls=%async_computation.3 | async-start | bytes 8388608
  155.0 5.8 %slice-start.3 = ((s8[16777216]{0:T(1024)(128)(4,1)}), s8[4194304]{0:T(1024)(128)(4,1)S(1)}, s32[]{:S(2)}) async-start(s8[16777216]{0:T(1024)(128)(4,1)} %bitcast.43), calls=%async_computation.4 | async-start | bytes 8388608
Sparse Core Ops, SparseCore 0:
  10.8 119.5 all-gather.3
